TPU v7x, 32 devices: a whole 2x2x4 slice. The times are simulated.
32 devices in a mesh: seq: 8 (over z, y), batch: 4 (over x, core).
Axes of the slice: x: 2, y: 2, z: 4, core: 2. Of those that a mesh axis runs over, the one named last changes fastest.
Arguments:
- conv_input: bfloat16 [4096, 8192], P(('batch', 'seq')), parts along dimension 0, may hold values from -6 to 6
- gate_input: bfloat16 [4096, 8192], P(('batch', 'seq')), parts along dimension 0, may hold values from -6 to 6
- conv_weight: bfloat16 [4, 8192], P(None, 'seq'), may hold values from -3 to 3
- conv_bias: bfloat16 [8192], P('seq'), may hold values from -3 to 3
- x_weight: bfloat16 [8192, 288], P('seq'), may hold values from -0.0625 to 0.0625
- dt_gain: float32 [256], replicated, may hold values from 0.5 to 1.5
- dt_weight: bfloat16 [256, 8192], P(None, 'seq'), may hold values from -0.375 to 0.375
- dt_bias: float32 [8192], P('seq'), may hold values from -6.9 to -2.3
- a_log: float32 [16, 8192], P(None, 'seq'), may hold values from 0 to 2.77
- skip: float32 [8192], P('seq'), may hold values from 0.5 to 1.5
Outputs:
- mixed: bfloat16 [4096, 8192], P(('batch', 'seq')), parts along dimension 0
There are 4 independent parts, one for each index of `batch`. A program takes and returns all parts, laid end to end along the dimension named above; an argument that names none is the same for every part. Nothing has to cross between parts.
All inputs are finite; a program needn't handle non-finite values.
Results may differ from a plain program's by a relative error of at most 0.0085.
Values may be sent and summed in bfloat16 or wider, within the bound.
A program may use at most 128 MiB of HBM per device.

v0:
```python
import jax
import jax.numpy as jnp
from jax import lax
from jax.sharding import PartitionSpec as P


def causal_conv(prefix, inputs, weight, bias):
    rows = inputs.shape[0]
    width = weight.shape[0]
    padded = jnp.concatenate([prefix, inputs.astype(jnp.float32)], 0)
    total = bias.astype(jnp.float32)[None, :]
    for tap in range(width):
        total = total + weight[tap].astype(jnp.float32)[None, :] * padded[tap : tap + rows]
    return jax.nn.silu(total).astype(jnp.bfloat16)


def link_blocks(earlier, later):
    return (earlier[0] * later[0], later[0] * earlier[1] + later[1])


def selective_scan(step, xfloat, bmat, cmat, rate):
    span = 16
    length, chans = step.shape
    states = rate.shape[0]
    blocks = length // span
    step_rows = step.reshape(blocks, span * chans)
    drive_rows = (step * xfloat).reshape(blocks, span * chans)
    b_rows = bmat.reshape(blocks, span * states)
    c_rows = cmat.reshape(blocks, span * states)
    state = jnp.zeros((blocks, states, chans), jnp.float32)
    running = jnp.zeros((blocks, chans), jnp.float32)
    local_parts = []
    elapsed = []
    for place in range(span):
        step_now = step_rows[:, place * chans : (place + 1) * chans]
        drive_now = drive_rows[:, place * chans : (place + 1) * chans]
        b_now = b_rows[:, place * states : (place + 1) * states]
        c_now = c_rows[:, place * states : (place + 1) * states]
        state = (
            jnp.exp(step_now[:, None, :] * rate[None]) * state
            + b_now[:, :, None] * drive_now[:, None, :]
        )
        local_parts.append(jnp.sum(c_now[:, :, None] * state, axis=1))
        running = running + step_now
        elapsed.append(running)
    totals = jnp.exp(running[:, None, :] * rate[None])
    _, through = lax.associative_scan(link_blocks, (totals, state), axis=0)
    starts = jnp.concatenate([jnp.zeros((1, states, chans), jnp.float32), through[: blocks - 1]], 0)
    pieces = []
    for place in range(span):
        c_now = c_rows[:, place * states : (place + 1) * states]
        carried = jnp.sum(
            c_now[:, :, None] * jnp.exp(elapsed[place][:, None, :] * rate[None]) * starts, axis=1
        )
        pieces.append(local_parts[place] + carried)
    return jnp.concatenate(pieces, 1).reshape(length, chans)


def local(
    conv_input,
    gate_input,
    conv_weight,
    conv_bias,
    x_weight,
    dt_gain,
    dt_weight,
    dt_bias,
    a_log,
    skip,
):
    width = conv_weight.shape[0]
    rank = dt_weight.shape[0]
    states = a_log.shape[0]
    arrived = lax.all_to_all(conv_input, "seq", split_axis=1, concat_axis=0, tiled=True)
    zero_prefix = jnp.zeros((width - 1, arrived.shape[1]), jnp.float32)
    conv_out = causal_conv(zero_prefix, arrived, conv_weight, conv_bias)
    partial_value = jnp.dot(conv_out, x_weight, preferred_element_type=jnp.float32)
    proj = lax.psum(partial_value, "seq")
    dt_low = proj[:, :rank]
    bmat = proj[:, rank : rank + states]
    cmat = proj[:, rank + states :]
    normed = (
        dt_low
        * lax.rsqrt(jnp.mean(dt_low * dt_low, axis=1, keepdims=True) + 1e-06)
        * dt_gain[None, :]
    ).astype(jnp.bfloat16)
    step = jax.nn.softplus(
        jnp.dot(normed, dt_weight, preferred_element_type=jnp.float32) + dt_bias[None, :]
    )
    rate = -jnp.exp(a_log)
    xfloat = conv_out.astype(jnp.float32)
    scanned = selective_scan(step, xfloat, bmat, cmat, rate)
    y_out = (scanned + skip[None, :] * xfloat).astype(jnp.bfloat16)
    returned = lax.all_to_all(y_out, "seq", split_axis=0, concat_axis=1, tiled=True)
    return (returned.astype(jnp.float32) * jax.nn.silu(gate_input.astype(jnp.float32))).astype(
        jnp.bfloat16
    )


def solution(mesh):
    return jax.shard_map(
        local,
        mesh=mesh,
        in_specs=(
            P(("batch", "seq"), None),
            P(("batch", "seq"), None),
            P(None, "seq"),
            P("seq"),
            P("seq", None),
            P(),
            P(None, "seq"),
            P("seq"),
            P(None, "seq"),
            P("seq"),
        ),
        out_specs=P(("batch", "seq"), None),
        check_vma=False,
    )
```

profile of v0, /device:TPU:0, one launch (start us, length us, event | category | flops | bytes accessed | tf_op | source)
XLA Modules:
  0.0 461.8 jit_solution(15684360439202959962)
XLA Ops:
  9.8 7.3 %all-to-all-start = ((bf16[128,8,1024]{2,0,1:T(8,128)(2,1)}), bf16[128,8,1024]{2,0,1:T(8,128)(2,1)S(1)}, u32[]{:S(2)}, u32[]{:S(2)}) async-start(bf16[128,8,1024]{2,0,1:T(8,128)(2,1)} %bitcast.22), calls=%async_computation | async-start | bytes 4194304 | tf_op jit(solution)/shard_map/all_to_all | solution.py:74
  17.2 48.1 %all-to-all-done = bf16[128,8,1024]{2,0,1:T(8,128)(2,1)S(1)} async-done(((bf16[128,8,1024]{2,0,1:T(8,128)(2,1)}), bf16[128,8,1024]{2,0,1:T(8,128)(2,1)S(1)}, u32[]{:S(2)}, u32[]{:S(2)}) %all-to-all-start) | async-done | bytes 2097184 | tf_op jit(solution)/shard_map/all_to_all | solution.py:74
  72.4 79.5 %all-reduce.16.cloned.1.call-done = f32[1024,288]{0,1:T(8,128)} async-done(((f32[1024,288]{0,1:T(8,128)}), f32[1024,288]{0,1:T(8,128)}) %all-reduce.16.cloned.1.call-update) | async-done | bytes 1179664 | tf_op jit(solution)/shard_map/psum | solution.py:78
  153.3 7.3 %convert_multiply_fusion.2 = (f32[1024,1024]{1,0:T(8,128)}, f32[1024,1024]{1,0:T(8,128)}) fusion(bf16[1024,1024]{1,0:T(8,128)(2,1)S(1)} %multiply_convert_fusion, f32[1024]{0:T(1024)S(1)} %copy-done.125, bf16[256,1024]{1,0:T(8,128)(2,1)S(1)} %copy-done.124, f32[1024,288]{0,1:T(8,128)} %all-reduce.16.cloned.1.call-done, f32[256]{0:T(256)S(1)} %copy-done.126, ...), kind=kOutput, calls=%fused_computation.4 | convolution fusion | flops 547094528 | bytes 12067840 | tf_op jit(solution)/shard_map/dot_general | solution.py:88
  160.6 5.0 %reshape.118 = f32[64,16384]{1,0:T(8,128)} reshape(f32[1024,1024]{1,0:T(8,128)} %get-tuple-element.143) | data formatting | bytes 8388608 | tf_op jit(solution)/shard_map/reshape | solution.py:26
  175.3 5.1 %reshape.120 = f32[64,16384]{1,0:T(8,128)} reshape(f32[1024,1024]{1,0:T(8,128)} %get-tuple-element.142) | data formatting | bytes 8388608 | tf_op jit(solution)/shard_map/reshape | solution.py:27
  184.2 23.0 %multiply_reduce_fusion.1 = (f32[64,1024]{1,0:T(8,128)}, f32[64,16,1024]{2,1,0:T(8,128)S(1)}, f32[64,16,1024]{2,1,0:T(8,128)}, f32[64,16,1024]{2,1,0:T(8,128)}) fusion(f32[64,16]{1,0:T(8,128)} %get-tuple-element.107, f32[64,1024]{1,0:T(8,128)} %get-tuple-element.75, f32[64,16]{1,0:T(8,128)} %get-tuple-element.123, f32[64,1024]{1,0:T(8,128)S(1)} %get-tuple-element.76, ...), kind=kLoop, calls=%fused_computation.13 | loop fusion | flops 69140480 | bytes 21368832 | tf_op jit(solution)/shard_map/reduce_sum | solution.py:43
  207.9 7.9 %multiply_reduce_fusion.3 = (f32[64,1024]{1,0:T(8,128)}, f32[64,1024]{1,0:T(8,128)}, f32[64,1024]{1,0:T(8,128)}, f32[64,16,1024]{2,1,0:T(8,128)S(1)}) fusion(f32[64,16]{1,0:T(8,128)S(1)} %get-tuple-element.108, f32[64,1024]{1,0:T(8,128)S(1)} %get-tuple-element.76, f32[64,16]{1,0:T(8,128)} %get-tuple-element.124, f32[64,1024]{1,0:T(8,128)S(1)} %get-tuple-element.77, ...), kind=kLoop, calls=%fused_computation.15 | loop fusion | flops 15532032 | bytes 10571776 | tf_op jit(solution)/shard_map/reduce_sum | solution.py:43
  236.3 5.7 %pad.46 = f32[16,16,1024]{2,1,0:T(8,128)} pad(f32[8,16,1024]{2,1,0:T(8,128)} %add.325, f32[]{:T(128)} %constant.4.clone.1), padding=1_0_1x0_0_0x0_0_0 | pad | bytes 1572868 | tf_op jit(solution)/shard_map/pad | solution.py:47
  246.6 7.0 %pad.47 = f32[32,16,1024]{2,1,0:T(8,128)S(1)} pad(f32[16,16,1024]{2,1,0:T(8,128)} %pad_maximum_fusion.1, f32[]{:T(128)} %constant.4.clone.1), padding=0_1_1x0_0_0x0_0_0 | pad | bytes 3145732 | tf_op jit(solution)/shard_map/pad | solution.py:47
  253.6 10.2 %pad.48 = f32[32,16,1024]{2,1,0:T(8,128)} pad(f32[16,16,1024]{2,1,0:T(8,128)} %add.327, f32[]{:T(128)} %constant.4.clone.1), padding=1_0_1x0_0_0x0_0_0 | pad | bytes 3145732 | tf_op jit(solution)/shard_map/pad | solution.py:47
  270.6 9.1 %multiply_reduce_fusion.17 = f32[64,1024]{1,0:T(8,128)} fusion(f32[64,16]{1,0:T(8,128)S(1)} %copy-done.96, f32[64,1024]{1,0:T(8,128)S(1)} %copy-done.68, f32[64,16]{1,0:T(8,128)S(1)} %copy-done.120, f32[64,1024]{1,0:T(8,128)S(1)} %copy-done.79, f32[16,1024]{1,0:T(8,128)S(1)} %exponential_negate_fusion, f32[64,1024]{1,0:T(8,128)S(1)} %copy-done.67, ...), kind=kLoop, calls=%fused_computation.29 | loop fusion | flops 35586048 | bytes 4558848 | tf_op jit(solution)/shard_map/reduce_sum | solution.py:43
  279.8 8.2 %multiply_reduce_fusion.19 = f32[64,1024]{1,0:T(8,128)} fusion(f32[64,16]{1,0:T(8,128)S(1)} %copy-done.98, f32[64,1024]{1,0:T(8,128)S(1)} %copy-done.67, f32[64,16]{1,0:T(8,128)S(1)} %copy-done.119, f32[64,1024]{1,0:T(8,128)S(1)} %copy-done.65, f32[64,16]{1,0:T(8,128)S(1)} %copy-done.118, f32[64,1024]{1,0:T(8,128)S(1)} %copy-done.77, ...), kind=kLoop, calls=%fused_computation.31 | loop fusion | flops 31391744 | bytes 4030464 | tf_op jit(solution)/shard_map/reduce_sum | solution.py:43
  287.9 7.0 %multiply_reduce_fusion.21 = f32[64,1024]{1,0:T(8,128)} fusion(f32[64,16]{1,0:T(8,128)S(1)} %copy-done.101, f32[64,1024]{1,0:T(8,128)S(1)} %copy-done.65, f32[64,16]{1,0:T(8,128)S(1)} %copy-done.118, f32[64,1024]{1,0:T(8,128)S(1)} %copy-done.77, f32[16,1024]{1,0:T(8,128)S(1)} %exponential_negate_fusion, f32[64,1024]{1,0:T(8,128)S(1)} %copy-done.57, ...), kind=kLoop, calls=%fused_computation.33 | loop fusion | flops 27197440 | bytes 3502080 | tf_op jit(solution)/shard_map/reduce_sum | solution.py:43
  296.4 18.5 %pad.62 = f32[63,16,1024]{2,1,0:T(8,128)} pad(f32[32,16,1024]{2,1,0:T(8,128)} %pad_maximum_fusion, f32[]{:T(128)} %constant.4.clone.1), padding=0_0_1x0_0_0x0_0_0 | pad | bytes 6225924 | tf_op jit(solution)/shard_map/slice | solution.py:48
  314.9 12.1 %pad.86 = f32[64,16,1024]{2,1,0:T(8,128)} pad(f32[32,16,1024]{2,1,0:T(8,128)S(1)} %copy-done.10, f32[]{:T(128)} %constant.4.clone.1), padding=1_0_1x0_0_0x0_0_0 | pad | bytes 6291460
  331.7 9.3 %multiply_reduce_fusion.29 = (f32[64,1024]{1,0:T(8,128)S(1)}, f32[64,1024]{1,0:T(8,128)S(1)}, f32[64,1024]{1,0:T(8,128)S(1)}, f32[64,1024]{1,0:T(8,128)S(1)}, f32[64,1024]{1,0:T(8,128)S(1)}, /*index=5*/f32[64,1024]{1,0:T(8,128)S(1)}) fusion(f32[64,16]{1,0:T(8,128)S(1)} %copy-done.106, f32[64,1024]{1,0:T(8,128)S(1)} %copy-done.62, ...), kind=kLoop, calls=%fused_computation.41 | loop fusion | flops 27918336 | bytes 7630848 | tf_op jit(solution)/shard_map/reduce_sum | solution.py:43
  341.9 7.3 %multiply_reduce_fusion.23 = (f32[64,1024]{1,0:T(8,128)S(1)}, f32[64,1024]{1,0:T(8,128)S(1)}, f32[64,1024]{1,0:T(8,128)S(1)}) fusion(f32[64,16]{1,0:T(8,128)S(1)} %copy-done.103, f32[64,1024]{1,0:T(8,128)S(1)} %copy-done.58, f32[64,16]{1,0:T(8,128)S(1)} %copy-done.110, f32[64,1024]{1,0:T(8,128)S(1)} %copy-done.60, f32[64,16]{1,0:T(8,128)S(1)} %copy-done.112, ...), kind=kLoop, calls=%fused_computation.35 | loop fusion | flops 27066368 | bytes 3506176 | tf_op jit(solution)/shard_map/reduce_sum | solution.py:43
  349.4 9.2 %multiply_reduce_fusion = (f32[64,1024]{1,0:T(8,128)S(1)}, f32[64,1024]{1,0:T(8,128)S(1)}, f32[64,1024]{1,0:T(8,128)S(1)}, f32[64,1024]{1,0:T(8,128)S(1)}, f32[64,1024]{1,0:T(8,128)S(1)}, /*index=5*/f32[64,1024]{1,0:T(8,128)S(1)}) fusion(f32[64,16]{1,0:T(8,128)S(1)} %copy-done.100, f32[16,1024]{1,0:T(8,128)S(1)} %exponential_negate_fusion, ...), kind=kLoop, calls=%fused_computation.12 | loop fusion | flops 24772608 | bytes 7364608 | tf_op jit(solution)/shard_map/reduce_sum | solution.py:52
  362.4 5.9 %multiply_reduce_fusion.9 = (f32[64,1024]{1,0:T(8,128)S(1)}, f32[64,1024]{1,0:T(8,128)S(1)}, f32[64,1024]{1,0:T(8,128)S(1)}, f32[64,1024]{1,0:T(8,128)S(1)}) fusion(f32[64,16]{1,0:T(8,128)S(1)} %copy-done.90, f32[64,1024]{1,0:T(8,128)S(1)} %copy-done.16, f32[64,16]{1,0:T(8,128)S(1)} %copy-done.86, f32[64,1024]{1,0:T(8,128)S(1)} %copy-done.26, ...), kind=kLoop, calls=%fused_computation.21 | loop fusion | flops 20709376 | bytes 6909952 | tf_op jit(solution)/shard_map/reduce_sum | solution.py:43
  368.4 9.0 %multiply_reduce_fusion.2 = (f32[64,1024]{1,0:T(8,128)S(1)}, f32[64,1024]{1,0:T(8,128)S(1)}, f32[64,1024]{1,0:T(8,128)S(1)}, f32[64,1024]{1,0:T(8,128)S(1)}, f32[64,1024]{1,0:T(8,128)S(1)}, /*index=5*/f32[64,1024]{1,0:T(8,128)S(1)}) fusion(f32[64,1024]{1,0:T(8,128)S(1)} %copy-done.33, f32[64,16]{1,0:T(8,128)S(1)} %copy-done.82, ...), kind=kLoop, calls=%fused_computation.14 | loop fusion | flops 24772608 | bytes 7364608 | tf_op jit(solution)/shard_map/reduce_sum | solution.py:52
  384.9 5.0 %reshape.121 = f32[1024,1024]{1,0:T(8,128)} reshape(f32[64,16384]{1,0:T(8,128)} %add_dynamic-update-slice_fusion) | data formatting | bytes 8388608 | tf_op jit(solution)/shard_map/reshape | solution.py:56
  389.9 9.1 %fusion.1 = bf16[1024,1024]{1,0:T(8,128)(2,1)S(1)} fusion(f32[1024,1024]{1,0:T(8,128)} %reshape.121, f32[1024]{0:T(1024)S(1)} %copy-done.122, f32[1024,1024]{1,0:T(8,128)} %bitcast.20, f32[1024]{0:T(1024)S(1)} %bitcast.30, f32[1024]{0:T(1024)S(1)} %bitcast.32, f32[1024]{0:T(1024)S(1)} %bitcast.28, f32[1024]{0:T(1024)S(1)} %bitcast.26, ...), kind=kLoop, calls=%fused_computation.6 | loop fusion | flops 17825792 | bytes 10510336 | tf_op jit(solution)/shard_map/convert_element_type | solution.py:93
  399.0 51.4 %all_to_all.26 = bf16[8,128,1024]{2,1,0:T(8,128)(2,1)S(1)} all-to-all(bf16[8,128,1024]{2,1,0:T(8,128)(2,1)S(1)} %bitcast.23), channel_id=1, replica_groups=mesh['seq'=8,'batch'=4] {'seq'}, dimensions={0} | all-to-all | bytes 4194304 | tf_op jit(solution)/shard_map/all_to_all | solution.py:94
  (325 shorter events, 79.7 us)
Async XLA Ops:
  6.5 63.9 %copy-start = (bf16[1024,288]{0,1:T(8,128)(2,1)S(1)}, bf16[1024,288]{0,1:T(8,128)(2,1)}, u32[]{:S(2)}) copy-start(bf16[1024,288]{0,1:T(8,128)(2,1)} %param.14) | copy-start | bytes 1769476
  9.8 55.5 %all-to-all-start = ((bf16[128,8,1024]{2,0,1:T(8,128)(2,1)}), bf16[128,8,1024]{2,0,1:T(8,128)(2,1)S(1)}, u32[]{:S(2)}, u32[]{:S(2)}) async-start(bf16[128,8,1024]{2,0,1:T(8,128)(2,1)} %bitcast.22), calls=%async_computation | async-start | bytes 4194304 | tf_op jit(solution)/shard_map/all_to_all | solution.py:74
  17.1 134.9 %all-reduce.16.cloned.1.call-start = ((), (), s32[]{:S(2)}) async-start(), calls=%async_computation.2 | async-start | bytes 2359296 | tf_op jit(solution)/shard_map/psum | solution.py:78
  17.2 48.6 %copy-start.94 = (f32[1,1024]{1,0:T(1,128)}, f32[1,1024]{1,0:T(1,128)S(1)}, u32[]{:S(2)}) copy-start(f32[1,1024]{1,0:T(1,128)S(1)} %get-tuple-element.141) | copy-start | bytes 12292
  70.5 82.8 %copy-start.124 = (bf16[256,1024]{1,0:T(8,128)(2,1)S(1)}, bf16[256,1024]{1,0:T(8,128)(2,1)}, u32[]{:S(2)}) copy-start(bf16[256,1024]{1,0:T(8,128)(2,1)} %param.16) | copy-start | bytes 1572868
  70.5 82.8 %copy-start.125 = (f32[1024]{0:T(1024)S(1)}, f32[1024]{0:T(1024)}, u32[]{:S(2)}) copy-start(f32[1024]{0:T(1024)} %param.17) | copy-start | bytes 12292
  70.5 82.8 %copy-start.126 = (f32[256]{0:T(256)S(1)}, f32[256]{0:T(256)}, u32[]{:S(2)}) copy-start(f32[256]{0:T(256)} %param.15) | copy-start | bytes 3076
  169.3 14.9 %copy-start.21 = (f32[64,1024]{1,0:T(8,128)}, f32[64,1024]{1,0:T(8,128)S(1)}, u32[]{:S(2)}) copy-start(f32[64,1024]{1,0:T(8,128)S(1)} %get-tuple-element.66) | copy-start | bytes 786436
  169.3 14.9 %copy-start.23 = (f32[64,1024]{1,0:T(8,128)}, f32[64,1024]{1,0:T(8,128)S(1)}, u32[]{:S(2)}) copy-start(f32[64,1024]{1,0:T(8,128)S(1)} %get-tuple-element.67) | copy-start | bytes 786436
  169.3 14.9 %copy-start.25 = (f32[64,1024]{1,0:T(8,128)}, f32[64,1024]{1,0:T(8,128)S(1)}, u32[]{:S(2)}) copy-start(f32[64,1024]{1,0:T(8,128)S(1)} %get-tuple-element.68) | copy-start | bytes 786436
  171.4 36.5 %copy-start.28 = (f32[64,1024]{1,0:T(8,128)}, f32[64,1024]{1,0:T(8,128)S(1)}, u32[]{:S(2)}) copy-start(f32[64,1024]{1,0:T(8,128)S(1)} %get-tuple-element.41) | copy-start | bytes 786436
  175.3 32.6 %copy-start.81 = (f32[64,16]{1,0:T(8,128)}, f32[64,16]{1,0:T(8,128)S(1)}, u32[]{:S(2)}) copy-start(f32[64,16]{1,0:T(8,128)S(1)} %get-tuple-element.108) | copy-start | bytes 12292
  184.1 23.1 %copy-start.15 = (f32[64,1024]{1,0:T(8,128)}, f32[64,1024]{1,0:T(8,128)S(1)}, u32[]{:S(2)}) copy-start(f32[64,1024]{1,0:T(8,128)S(1)} %get-tuple-element.79) | copy-start | bytes 786436
  184.1 23.1 %copy-start.17 = (f32[64,1024]{1,0:T(8,128)}, f32[64,1024]{1,0:T(8,128)S(1)}, u32[]{:S(2)}) copy-start(f32[64,1024]{1,0:T(8,128)S(1)} %get-tuple-element.80) | copy-start | bytes 786436
  184.1 23.1 %copy-start.19 = (f32[64,1024]{1,0:T(8,128)}, f32[64,1024]{1,0:T(8,128)S(1)}, u32[]{:S(2)}) copy-start(f32[64,1024]{1,0:T(8,128)S(1)} %get-tuple-element.81) | copy-start | bytes 786436
  184.1 23.1 %copy-start.54 = (f32[64,1024]{1,0:T(8,128)}, f32[64,1024]{1,0:T(8,128)S(1)}, u32[]{:S(2)}) copy-start(f32[64,1024]{1,0:T(8,128)S(1)} %get-tuple-element.74) | copy-start | bytes 786436
  294.9 19.9 %copy-start.10 = (f32[32,16,1024]{2,1,0:T(8,128)S(1)}, f32[32,16,1024]{2,1,0:T(8,128)}, u32[]{:S(2)}) copy-start(f32[32,16,1024]{2,1,0:T(8,128)} %add.329) | copy-start | bytes 6291460
  349.3 13.1 %copy-start.13 = (f32[64,16,1024]{2,1,0:T(8,128)S(1)}, f32[64,16,1024]{2,1,0:T(8,128)}, u32[]{:S(2)}) copy-start(f32[64,16,1024]{2,1,0:T(8,128)} %get-tuple-element.40) | copy-start | bytes 12582916
  349.3 13.1 %copy-start.16 = (f32[64,1024]{1,0:T(8,128)S(1)}, f32[64,1024]{1,0:T(8,128)}, u32[]{:S(2)}) copy-start(f32[64,1024]{1,0:T(8,128)} %copy-done.15) | copy-start | bytes 786436
  349.3 13.1 %copy-start.18 = (f32[64,1024]{1,0:T(8,128)S(1)}, f32[64,1024]{1,0:T(8,128)}, u32[]{:S(2)}) copy-start(f32[64,1024]{1,0:T(8,128)} %copy-done.17) | copy-start | bytes 786436
  349.3 13.1 %copy-start.20 = (f32[64,1024]{1,0:T(8,128)S(1)}, f32[64,1024]{1,0:T(8,128)}, u32[]{:S(2)}) copy-start(f32[64,1024]{1,0:T(8,128)} %copy-done.19) | copy-start | bytes 786436
  349.3 13.1 %copy-start.22 = (f32[64,1024]{1,0:T(8,128)S(1)}, f32[64,1024]{1,0:T(8,128)}, u32[]{:S(2)}) copy-start(f32[64,1024]{1,0:T(8,128)} %copy-done.21) | copy-start | bytes 786436
  349.3 13.1 %copy-start.24 = (f32[64,1024]{1,0:T(8,128)S(1)}, f32[64,1024]{1,0:T(8,128)}, u32[]{:S(2)}) copy-start(f32[64,1024]{1,0:T(8,128)} %copy-done.23) | copy-start | bytes 786436
  349.3 13.1 %copy-start.26 = (f32[64,1024]{1,0:T(8,128)S(1)}, f32[64,1024]{1,0:T(8,128)}, u32[]{:S(2)}) copy-start(f32[64,1024]{1,0:T(8,128)} %copy-done.25) | copy-start | bytes 786436
  (105 other events, 630.9 us)
Sparse Core Ops, SparseCore 0:
  72.5 79.4 all-reduce.15
where the time goes:
time: 465 us; the launch traced here: 462 us
  other arithmetic  151 us (32%)
  waiting for transfers between devices  128 us (28%)
  local copies, waits for them, and re-layouts  100 us (22%)
  blocking collectives  51.4 us (11%)
  between operations  15 us (3%)
  matrix products  9.11 us (2%)
  starting transfers between devices  7.35 us (2%)
    psum x1, waiting for transfers between devices, local(): proj = lax.psum(partial_value, 'seq')  79.5 us
    reduce_sum x8, other arithmetic, selective_scan(): local_parts.append(jnp.sum(c_now[:, :, None] * state, axis=1))  77.7 us
    all_to_all x1, blocking collectives, local(): lax.all_to_all(y_out, 'seq', split_axis=0, concat_axis=1, tiled=True)  51.4 us
    all_to_all x1, waiting for transfers between devices, local(): lax.all_to_all(conv_input, 'seq', split_axis=1, concat_axis=0, tiled=True)  48.1 us
    pad x8, local copies, waits for them, and re-layouts, selective_scan(): _, through = lax.associative_scan(link_blocks, (totals, state), axis=0)  31.3 us
    slice x1, local copies, waits for them, and re-layouts, selective_scan(): through[:blocks - 1]  18.5 us
    unnamed x255, local copies, waits for them, and re-layouts  18.3 us
    reduce_sum x2, other arithmetic, selective_scan(): jnp.sum(c_now[:, :, None] * jnp.exp(elapsed[place][:, None, :] * rate[Non...  18.2 us
  transfers between devices with their start and end apart: 2, of which 2 were waited for; matrix products, arithmetic and copies ran while one was open for 0% of the time, Pallas kernels for 0%

commit v1 on v0

--- a/solution.py
+++ b/solution.py
@@ -75,7 +75,7 @@
     zero_prefix = jnp.zeros((width - 1, arrived.shape[1]), jnp.float32)
     conv_out = causal_conv(zero_prefix, arrived, conv_weight, conv_bias)
     partial_value = jnp.dot(conv_out, x_weight, preferred_element_type=jnp.float32)
-    proj = lax.psum(partial_value, "seq")
+    proj = jnp.sum(lax.all_gather(partial_value, "seq"), axis=0)
     dt_low = proj[:, :rank]
     bmat = proj[:, rank : rank + states]
     cmat = proj[:, rank + states :]

time: 465 us -> 536 us (1.15)
  waiting for transfers between devices: 128 us -> 185 us
  local copies, waits for them, and re-layouts: 100 us -> 112 us
    all_gather x0 -> x1, waiting for transfers between devices: none -> 136 us  [local(): proj = jnp.sum(lax.all_gather(partial_value, 'seq'), axis=0)]
    psum x1 -> x0, waiting for transfers between devices: 79.5 us -> none  [local(): proj = lax.psum(partial_value, 'seq')]
    unnamed x255 -> x256, local copies, waits for them, and re-layouts: 18.3 us -> 30.6 us
where the time goes in v1:
time: 536 us; the launch traced here: 530 us
  waiting for transfers between devices  185 us (35%)
  other arithmetic  153 us (29%)
  local copies, waits for them, and re-layouts  112 us (21%)
  blocking collectives  50.8 us (9%)
  between operations  15.3 us (3%)
  matrix products  7.91 us (1%)
  starting transfers between devices  7.35 us (1%)
    all_gather x1, waiting for transfers between devices, local(): proj = jnp.sum(lax.all_gather(partial_value, 'seq'), axis=0)  136 us
    reduce_sum x8, other arithmetic, selective_scan(): local_parts.append(jnp.sum(c_now[:, :, None] * state, axis=1))  77.7 us
    all_to_all x1, blocking collectives, local(): lax.all_to_all(y_out, 'seq', split_axis=0, concat_axis=1, tiled=True)  50.8 us
    all_to_all x1, waiting for transfers between devices, local(): lax.all_to_all(conv_input, 'seq', split_axis=1, concat_axis=0, tiled=True)  48.1 us
    pad x8, local copies, waits for them, and re-layouts, selective_scan(): _, through = lax.associative_scan(link_blocks, (totals, state), axis=0)  31.5 us
    unnamed x256, local copies, waits for them, and re-layouts  30.6 us
    slice x1, local copies, waits for them, and re-layouts, selective_scan(): through[:blocks - 1]  18.5 us
    reduce_sum x2, other arithmetic, selective_scan(): jnp.sum(c_now[:, :, None] * jnp.exp(elapsed[place][:, None, :] * rate[Non...  18 us
  transfers between devices with their start and end apart: 2, of which 2 were waited for; matrix products, arithmetic and copies ran while one was open for 0% of the time, Pallas kernels for 0%

profile of v1, /device:TPU:0, one launch (start us, length us, event | category | flops | bytes accessed | tf_op | source)
XLA Modules:
  0.0 530.3 jit_solution(9766599887796713287)
XLA Ops:
  9.8 7.3 %all-to-all-start = ((bf16[128,8,1024]{2,0,1:T(8,128)(2,1)}), bf16[128,8,1024]{2,0,1:T(8,128)(2,1)S(1)}, u32[]{:S(2)}, u32[]{:S(2)}) async-start(bf16[128,8,1024]{2,0,1:T(8,128)(2,1)} %bitcast.28), calls=%async_computation | async-start | bytes 4194304 | tf_op jit(solution)/shard_map/all_to_all | solution.py:74
  17.2 48.1 %all-to-all-done = bf16[128,8,1024]{2,0,1:T(8,128)(2,1)S(1)} async-done(((bf16[128,8,1024]{2,0,1:T(8,128)(2,1)}), bf16[128,8,1024]{2,0,1:T(8,128)(2,1)S(1)}, u32[]{:S(2)}, u32[]{:S(2)}) %all-to-all-start) | async-done | bytes 2097184 | tf_op jit(solution)/shard_map/all_to_all | solution.py:74
  72.9 136.4 %all-gather.3.cloned.1.call-done = f32[8192,288]{0,1:T(8,128)} async-done(((f32[1024,288]{0,1:T(8,128)}), f32[8192,288]{0,1:T(8,128)}) %all-gather.3.cloned.1.call-update) | async-done | bytes 9437200 | tf_op jit(solution)/shard_map/all_gather | solution.py:78
  209.3 12.3 %copy.25 = f32[36,8,8,1024]{3,2,1,0:T(8,128)S(1)} copy(f32[36,8,8,1024]{3,1,2,0:T(8,128)} %bitcast.27) | data formatting | bytes 18874368
  224.3 6.1 %convert_multiply_fusion.2 = (f32[1024,1024]{1,0:T(8,128)}, f32[1024,1024]{1,0:T(8,128)}) fusion(bf16[1024,1024]{1,0:T(8,128)(2,1)S(1)} %multiply_convert_fusion, f32[1024]{0:T(1024)S(1)} %copy-done.125, bf16[256,1024]{1,0:T(8,128)(2,1)S(1)} %copy-done.124, f32[1024,288]{0,1:T(8,128)S(1)} %bitcast_reduce_fusion, f32[256]{0:T(256)S(1)} %copy-done.126, ...), kind=kOutput, calls=%fused_computation.5 | convolution fusion | flops 547094528 | bytes 12067840 | tf_op jit(solution)/shard_map/dot_general | solution.py:88
  244.0 5.1 reshape.120
  252.9 23.0 %multiply_reduce_fusion.1 = (f32[64,1024]{1,0:T(8,128)}, f32[64,16,1024]{2,1,0:T(8,128)S(1)}, f32[64,16,1024]{2,1,0:T(8,128)}, f32[64,16,1024]{2,1,0:T(8,128)}) fusion(f32[64,16]{1,0:T(8,128)} %get-tuple-element.107, f32[64,1024]{1,0:T(8,128)} %get-tuple-element.75, f32[64,16]{1,0:T(8,128)} %get-tuple-element.123, f32[64,1024]{1,0:T(8,128)S(1)} %get-tuple-element.76, ...), kind=kLoop, calls=%fused_computation.14 | loop fusion | flops 69140480 | bytes 21368832 | tf_op jit(solution)/shard_map/reduce_sum | solution.py:43
  276.6 7.8 %multiply_reduce_fusion.3 = (f32[64,1024]{1,0:T(8,128)}, f32[64,1024]{1,0:T(8,128)}, f32[64,1024]{1,0:T(8,128)}, f32[64,16,1024]{2,1,0:T(8,128)S(1)}) fusion(f32[64,16]{1,0:T(8,128)S(1)} %get-tuple-element.108, f32[64,1024]{1,0:T(8,128)S(1)} %get-tuple-element.76, f32[64,16]{1,0:T(8,128)} %get-tuple-element.124, f32[64,1024]{1,0:T(8,128)S(1)} %get-tuple-element.77, ...), kind=kLoop, calls=%fused_computation.16 | loop fusion | flops 15532032 | bytes 10571776 | tf_op jit(solution)/shard_map/reduce_sum | solution.py:43
  304.8 5.9 %pad.46 = f32[16,16,1024]{2,1,0:T(8,128)} pad(f32[8,16,1024]{2,1,0:T(8,128)} %add.323, f32[]{:T(128)} %constant.4.clone.1), padding=1_0_1x0_0_0x0_0_0 | pad | bytes 1572868 | tf_op jit(solution)/shard_map/pad | solution.py:47
  315.4 7.0 %pad.47 = f32[32,16,1024]{2,1,0:T(8,128)S(1)} pad(f32[16,16,1024]{2,1,0:T(8,128)} %pad_maximum_fusion.1, f32[]{:T(128)} %constant.4.clone.1), padding=0_1_1x0_0_0x0_0_0 | pad | bytes 3145732 | tf_op jit(solution)/shard_map/pad | solution.py:47
  322.3 10.2 %pad.48 = f32[32,16,1024]{2,1,0:T(8,128)} pad(f32[16,16,1024]{2,1,0:T(8,128)} %add.325, f32[]{:T(128)} %constant.4.clone.1), padding=1_0_1x0_0_0x0_0_0 | pad | bytes 3145732 | tf_op jit(solution)/shard_map/pad | solution.py:47
  339.4 9.1 %multiply_reduce_fusion.17 = f32[64,1024]{1,0:T(8,128)} fusion(f32[64,16]{1,0:T(8,128)S(1)} %copy-done.96, f32[64,1024]{1,0:T(8,128)S(1)} %copy-done.68, f32[64,16]{1,0:T(8,128)S(1)} %copy-done.120, f32[64,1024]{1,0:T(8,128)S(1)} %copy-done.79, f32[16,1024]{1,0:T(8,128)S(1)} %exponential_negate_fusion, f32[64,1024]{1,0:T(8,128)S(1)} %copy-done.67, ...), kind=kLoop, calls=%fused_computation.30 | loop fusion | flops 35586048 | bytes 4558848 | tf_op jit(solution)/shard_map/reduce_sum | solution.py:43
  348.5 8.2 %multiply_reduce_fusion.19 = f32[64,1024]{1,0:T(8,128)} fusion(f32[64,16]{1,0:T(8,128)S(1)} %copy-done.98, f32[64,1024]{1,0:T(8,128)S(1)} %copy-done.67, f32[64,16]{1,0:T(8,128)S(1)} %copy-done.119, f32[64,1024]{1,0:T(8,128)S(1)} %copy-done.65, f32[64,16]{1,0:T(8,128)S(1)} %copy-done.118, f32[64,1024]{1,0:T(8,128)S(1)} %copy-done.77, ...), kind=kLoop, calls=%fused_computation.32 | loop fusion | flops 31391744 | bytes 4030464 | tf_op jit(solution)/shard_map/reduce_sum | solution.py:43
  356.6 7.0 %multiply_reduce_fusion.21 = f32[64,1024]{1,0:T(8,128)} fusion(f32[64,16]{1,0:T(8,128)S(1)} %copy-done.101, f32[64,1024]{1,0:T(8,128)S(1)} %copy-done.65, f32[64,16]{1,0:T(8,128)S(1)} %copy-done.118, f32[64,1024]{1,0:T(8,128)S(1)} %copy-done.77, f32[16,1024]{1,0:T(8,128)S(1)} %exponential_negate_fusion, f32[64,1024]{1,0:T(8,128)S(1)} %copy-done.57, ...), kind=kLoop, calls=%fused_computation.34 | loop fusion | flops 27197440 | bytes 3502080 | tf_op jit(solution)/shard_map/reduce_sum | solution.py:43
  365.1 18.5 %pad.62 = f32[63,16,1024]{2,1,0:T(8,128)} pad(f32[32,16,1024]{2,1,0:T(8,128)} %pad_maximum_fusion, f32[]{:T(128)} %constant.4.clone.1), padding=0_0_1x0_0_0x0_0_0 | pad | bytes 6225924 | tf_op jit(solution)/shard_map/slice | solution.py:48
  383.6 12.1 %pad.86 = f32[64,16,1024]{2,1,0:T(8,128)} pad(f32[32,16,1024]{2,1,0:T(8,128)S(1)} %copy-done.10, f32[]{:T(128)} %constant.4.clone.1), padding=1_0_1x0_0_0x0_0_0 | pad | bytes 6291460
  400.4 9.3 %multiply_reduce_fusion.29 = (f32[64,1024]{1,0:T(8,128)S(1)}, f32[64,1024]{1,0:T(8,128)S(1)}, f32[64,1024]{1,0:T(8,128)S(1)}, f32[64,1024]{1,0:T(8,128)S(1)}, f32[64,1024]{1,0:T(8,128)S(1)}, /*index=5*/f32[64,1024]{1,0:T(8,128)S(1)}) fusion(f32[64,16]{1,0:T(8,128)S(1)} %copy-done.106, f32[64,1024]{1,0:T(8,128)S(1)} %copy-done.62, ...), kind=kLoop, calls=%fused_computation.42 | loop fusion | flops 27918336 | bytes 7630848 | tf_op jit(solution)/shard_map/reduce_sum | solution.py:43
  410.6 7.3 %multiply_reduce_fusion.23 = (f32[64,1024]{1,0:T(8,128)S(1)}, f32[64,1024]{1,0:T(8,128)S(1)}, f32[64,1024]{1,0:T(8,128)S(1)}) fusion(f32[64,16]{1,0:T(8,128)S(1)} %copy-done.103, f32[64,1024]{1,0:T(8,128)S(1)} %copy-done.58, f32[64,16]{1,0:T(8,128)S(1)} %copy-done.110, f32[64,1024]{1,0:T(8,128)S(1)} %copy-done.60, f32[64,16]{1,0:T(8,128)S(1)} %copy-done.112, ...), kind=kLoop, calls=%fused_computation.36 | loop fusion | flops 27066368 | bytes 3506176 | tf_op jit(solution)/shard_map/reduce_sum | solution.py:43
  418.1 9.0 %multiply_reduce_fusion = (f32[64,1024]{1,0:T(8,128)S(1)}, f32[64,1024]{1,0:T(8,128)S(1)}, f32[64,1024]{1,0:T(8,128)S(1)}, f32[64,1024]{1,0:T(8,128)S(1)}, f32[64,1024]{1,0:T(8,128)S(1)}, /*index=5*/f32[64,1024]{1,0:T(8,128)S(1)}) fusion(f32[64,16]{1,0:T(8,128)S(1)} %copy-done.100, f32[16,1024]{1,0:T(8,128)S(1)} %exponential_negate_fusion, ...), kind=kLoop, calls=%fused_computation.13 | loop fusion | flops 24772608 | bytes 7364608 | tf_op jit(solution)/shard_map/reduce_sum | solution.py:52
  430.9 6.1 %multiply_reduce_fusion.9 = (f32[64,1024]{1,0:T(8,128)S(1)}, f32[64,1024]{1,0:T(8,128)S(1)}, f32[64,1024]{1,0:T(8,128)S(1)}, f32[64,1024]{1,0:T(8,128)S(1)}) fusion(f32[64,16]{1,0:T(8,128)S(1)} %copy-done.90, f32[64,1024]{1,0:T(8,128)S(1)} %copy-done.16, f32[64,16]{1,0:T(8,128)S(1)} %copy-done.86, f32[64,1024]{1,0:T(8,128)S(1)} %copy-done.26, ...), kind=kLoop, calls=%fused_computation.22 | loop fusion | flops 20709376 | bytes 6909952 | tf_op jit(solution)/shard_map/reduce_sum | solution.py:43
  437.2 9.0 %multiply_reduce_fusion.2 = (f32[64,1024]{1,0:T(8,128)S(1)}, f32[64,1024]{1,0:T(8,128)S(1)}, f32[64,1024]{1,0:T(8,128)S(1)}, f32[64,1024]{1,0:T(8,128)S(1)}, f32[64,1024]{1,0:T(8,128)S(1)}, /*index=5*/f32[64,1024]{1,0:T(8,128)S(1)}) fusion(f32[64,1024]{1,0:T(8,128)S(1)} %copy-done.33, f32[64,16]{1,0:T(8,128)S(1)} %copy-done.82, ...), kind=kLoop, calls=%fused_computation.15 | loop fusion | flops 24772608 | bytes 7364608 | tf_op jit(solution)/shard_map/reduce_sum | solution.py:52
  453.6 5.0 reshape.121
  458.7 9.1 %fusion.1 = bf16[1024,1024]{1,0:T(8,128)(2,1)S(1)} fusion(f32[1024,1024]{1,0:T(8,128)} %reshape.121, f32[1024]{0:T(1024)S(1)} %copy-done.122, f32[1024,1024]{1,0:T(8,128)} %bitcast.25, f32[1024]{0:T(1024)S(1)} %bitcast.36, f32[1024]{0:T(1024)S(1)} %bitcast.38, f32[1024]{0:T(1024)S(1)} %bitcast.34, f32[1024]{0:T(1024)S(1)} %bitcast.32, ...), kind=kLoop, calls=%fused_computation.7 | loop fusion | flops 17825792 | bytes 10510336 | tf_op jit(solution)/shard_map/convert_element_type | solution.py:93
  467.8 50.8 %all_to_all.26 = bf16[8,128,1024]{2,1,0:T(8,128)(2,1)S(1)} all-to-all(bf16[8,128,1024]{2,1,0:T(8,128)(2,1)S(1)} %bitcast.29), channel_id=1, replica_groups=mesh['seq'=8,'batch'=4] {'seq'}, dimensions={0} | all-to-all | bytes 4194304 | tf_op jit(solution)/shard_map/all_to_all | solution.py:94
  (327 shorter events, 85.4 us)
Async XLA Ops:
  6.5 64.4 %copy-start = (bf16[1024,288]{0,1:T(8,128)(2,1)S(1)}, bf16[1024,288]{0,1:T(8,128)(2,1)}, u32[]{:S(2)}) copy-start(bf16[1024,288]{0,1:T(8,128)(2,1)} %param.14) | copy-start | bytes 1769476
  9.8 55.5 %all-to-all-start = ((bf16[128,8,1024]{2,0,1:T(8,128)(2,1)}), bf16[128,8,1024]{2,0,1:T(8,128)(2,1)S(1)}, u32[]{:S(2)}, u32[]{:S(2)}) async-start(bf16[128,8,1024]{2,0,1:T(8,128)(2,1)} %bitcast.28), calls=%async_computation | async-start | bytes 4194304 | tf_op jit(solution)/shard_map/all_to_all | solution.py:74
  17.1 192.2 %all-gather.3.cloned.1.call-start = ((), (), s32[]{:S(2)}) async-start(), calls=%async_computation.2 | async-start | bytes 10616832 | tf_op jit(solution)/shard_map/all_gather | solution.py:78
  17.2 48.6 %copy-start.94 = (f32[1,1024]{1,0:T(1,128)}, f32[1,1024]{1,0:T(1,128)S(1)}, u32[]{:S(2)}) copy-start(f32[1,1024]{1,0:T(1,128)S(1)} %get-tuple-element.141) | copy-start | bytes 12292
  239.0 13.8 %copy-start.21 = (f32[64,1024]{1,0:T(8,128)}, f32[64,1024]{1,0:T(8,128)S(1)}, u32[]{:S(2)}) copy-start(f32[64,1024]{1,0:T(8,128)S(1)} %get-tuple-element.66) | copy-start | bytes 786436
  239.0 13.8 %copy-start.23 = (f32[64,1024]{1,0:T(8,128)}, f32[64,1024]{1,0:T(8,128)S(1)}, u32[]{:S(2)}) copy-start(f32[64,1024]{1,0:T(8,128)S(1)} %get-tuple-element.67) | copy-start | bytes 786436
  239.0 13.8 %copy-start.25 = (f32[64,1024]{1,0:T(8,128)}, f32[64,1024]{1,0:T(8,128)S(1)}, u32[]{:S(2)}) copy-start(f32[64,1024]{1,0:T(8,128)S(1)} %get-tuple-element.68) | copy-start | bytes 786436
  241.2 35.4 %copy-start.29 = (f32[64,1024]{1,0:T(8,128)}, f32[64,1024]{1,0:T(8,128)S(1)}, u32[]{:S(2)}) copy-start(f32[64,1024]{1,0:T(8,128)S(1)} %get-tuple-element.41) | copy-start | bytes 786436
  244.0 32.6 %copy-start.81 = (f32[64,16]{1,0:T(8,128)}, f32[64,16]{1,0:T(8,128)S(1)}, u32[]{:S(2)}) copy-start(f32[64,16]{1,0:T(8,128)S(1)} %get-tuple-element.108) | copy-start | bytes 12292
  252.8 23.1 %copy-start.15 = (f32[64,1024]{1,0:T(8,128)}, f32[64,1024]{1,0:T(8,128)S(1)}, u32[]{:S(2)}) copy-start(f32[64,1024]{1,0:T(8,128)S(1)} %get-tuple-element.79) | copy-start | bytes 786436
  252.8 23.1 %copy-start.17 = (f32[64,1024]{1,0:T(8,128)}, f32[64,1024]{1,0:T(8,128)S(1)}, u32[]{:S(2)}) copy-start(f32[64,1024]{1,0:T(8,128)S(1)} %get-tuple-element.80) | copy-start | bytes 786436
  252.8 23.1 %copy-start.19 = (f32[64,1024]{1,0:T(8,128)}, f32[64,1024]{1,0:T(8,128)S(1)}, u32[]{:S(2)}) copy-start(f32[64,1024]{1,0:T(8,128)S(1)} %get-tuple-element.81) | copy-start | bytes 786436
  252.8 23.1 %copy-start.54 = (f32[64,1024]{1,0:T(8,128)}, f32[64,1024]{1,0:T(8,128)S(1)}, u32[]{:S(2)}) copy-start(f32[64,1024]{1,0:T(8,128)S(1)} %get-tuple-element.74) | copy-start | bytes 786436
  363.7 19.9 %copy-start.10 = (f32[32,16,1024]{2,1,0:T(8,128)S(1)}, f32[32,16,1024]{2,1,0:T(8,128)}, u32[]{:S(2)}) copy-start(f32[32,16,1024]{2,1,0:T(8,128)} %add.327) | copy-start | bytes 6291460
  418.0 12.9 %copy-start.13 = (f32[64,16,1024]{2,1,0:T(8,128)S(1)}, f32[64,16,1024]{2,1,0:T(8,128)}, u32[]{:S(2)}) copy-start(f32[64,16,1024]{2,1,0:T(8,128)} %get-tuple-element.40) | copy-start | bytes 12582916
  418.0 12.8 %copy-start.16 = (f32[64,1024]{1,0:T(8,128)S(1)}, f32[64,1024]{1,0:T(8,128)}, u32[]{:S(2)}) copy-start(f32[64,1024]{1,0:T(8,128)} %copy-done.15) | copy-start | bytes 786436
  418.0 12.8 %copy-start.18 = (f32[64,1024]{1,0:T(8,128)S(1)}, f32[64,1024]{1,0:T(8,128)}, u32[]{:S(2)}) copy-start(f32[64,1024]{1,0:T(8,128)} %copy-done.17) | copy-start | bytes 786436
  418.0 12.8 %copy-start.20 = (f32[64,1024]{1,0:T(8,128)S(1)}, f32[64,1024]{1,0:T(8,128)}, u32[]{:S(2)}) copy-start(f32[64,1024]{1,0:T(8,128)} %copy-done.19) | copy-start | bytes 786436
  418.0 12.8 %copy-start.22 = (f32[64,1024]{1,0:T(8,128)S(1)}, f32[64,1024]{1,0:T(8,128)}, u32[]{:S(2)}) copy-start(f32[64,1024]{1,0:T(8,128)} %copy-done.21) | copy-start | bytes 786436
  418.0 12.8 %copy-start.24 = (f32[64,1024]{1,0:T(8,128)S(1)}, f32[64,1024]{1,0:T(8,128)}, u32[]{:S(2)}) copy-start(f32[64,1024]{1,0:T(8,128)} %copy-done.23) | copy-start | bytes 786436
  418.1 12.8 %copy-start.26 = (f32[64,1024]{1,0:T(8,128)S(1)}, f32[64,1024]{1,0:T(8,128)}, u32[]{:S(2)}) copy-start(f32[64,1024]{1,0:T(8,128)} %copy-done.25) | copy-start | bytes 786436
  418.1 12.8 %copy-start.80 = (f32[64,16]{1,0:T(8,128)S(1)}, f32[64,16]{1,0:T(8,128)}, u32[]{:S(2)}) copy-start(f32[64,16]{1,0:T(8,128)} %get-tuple-element.106) | copy-start | bytes 12292
  418.1 12.8 %copy-start.83 = (f32[64,16]{1,0:T(8,128)S(1)}, f32[64,16]{1,0:T(8,128)}, u32[]{:S(2)}) copy-start(f32[64,16]{1,0:T(8,128)} %get-tuple-element.112) | copy-start | bytes 12292
  418.1 12.8 %copy-start.84 = (f32[64,16]{1,0:T(8,128)S(1)}, f32[64,16]{1,0:T(8,128)}, u32[]{:S(2)}) copy-start(f32[64,16]{1,0:T(8,128)} %get-tuple-element.113) | copy-start | bytes 12292
  (105 other events, 597.6 us)
Sparse Core Ops, SparseCore 0:
  73.0 136.2 all-gather.2
